TPU v7x, 32 devices: a whole 2x2x4 slice. The times are simulated.
32 devices in a mesh: row: 4 (over z), col: 8 (over y, x, core).
Axes of the slice: x: 2, y: 2, z: 4, core: 2. Of those that a mesh axis runs over, the one named last changes fastest.
Arguments:
- a_matrix: float32 [8192, 8192], P('row', 'col'), may hold values from -14 to 30, as said below
- b_matrix: float32 [4096, 4096], P('row', 'col'), may hold values from -14 to 30, as said below
- c_matrix: float32 [8192, 4096], P('row', 'col'), may hold values from -6 to 6
Outputs:
- a_swept: float32 [8192, 8192], P('row', 'col')
- c_swept: float32 [8192, 4096], P('row', 'col')
- b_next: float32 [4096, 4096], P('row', 'col')
Inputs may be any that keep to these rules, and one draw needn't show every extreme that they name: `a_matrix`: symmetric positive definite; its smallest eigenvalue is at least 1. `b_matrix`: symmetric positive definite; its smallest eigenvalue is at least 1.
All inputs are finite; a program needn't handle non-finite values. Where the computation divides by a largest or mean magnitude, that divisor is 1e-20 or more.
Results may differ from a plain program's by a relative error of at most 0.00012.
Values sent between devices are 32-bit elements; how exact they have to be, the bound alone decides.
No kernel may reach another device: no remote copies, remote signals or barrier semaphores. Data moves between devices by JAX's collectives and lax.ppermute only.
A program may use at most 128 MiB of HBM per device.

v0:
```python
import jax
import jax.numpy as jnp
from jax import lax
from jax.sharding import PartitionSpec as P

PANEL = 256
PIVOT_ITERS = 6
STEPS_A = 2
STEPS_B = 16
EXACT = lax.Precision.HIGHEST
CLOSE = lax.Precision.HIGH


def spread(value, axis, source):
    kept = jnp.where(lax.axis_index(axis) == source, value, 0).astype(value.dtype)
    return lax.psum(kept, axis)


def pivot_inverse(pivot):
    order = pivot.shape[0]
    unit_square = jnp.eye(order, dtype=jnp.float32)
    scaling = 1.0 / jnp.sqrt(jnp.sum(pivot * unit_square, axis=1))
    unit = pivot * scaling[:, None] * scaling[None, :]
    ceiling = jnp.max(jnp.sum(jnp.abs(unit), axis=1))
    approx = jnp.eye(order, dtype=jnp.float32) / ceiling
    for turn in range(PIVOT_ITERS):
        product = jnp.dot(unit, approx, precision=EXACT, preferred_element_type=jnp.float32)
        approx = 2.0 * approx - jnp.dot(
            approx, product, precision=EXACT, preferred_element_type=jnp.float32
        )
    return approx * scaling[:, None] * scaling[None, :]


def mul(left, right, dims, precision):
    return lax.dot_general(
        left, right, (dims, ((), ())), precision=precision, preferred_element_type=jnp.float32
    )


def sweep_panel(block, panel, places):
    order = block.shape[0]
    index = jnp.arange(order, dtype=jnp.int32)
    eye = (index[:, None] == jnp.concatenate([index, places])[None, :]).astype(jnp.float32)
    both = jnp.concatenate([block, panel], 1)
    for start in range(0, order, PANEL):
        stop = start + PANEL
        inverse = pivot_inverse(both[start:stop, start:stop].T)
        solved = mul(inverse, both[start:stop] - eye[start:stop], ((0,), (0,)), EXACT)
        updated = both - mul(both[:, start:stop], solved, ((1,), (0,)), CLOSE)
        both = jnp.concatenate([updated[:start], eye[start:stop] - solved, updated[stop:]], 0)
    return (both[:, order:], eye[:, order:])


def a_sweep(matrix, other):
    local_rows, local_cols = matrix.shape
    other_cols = other.shape[1]
    order = STEPS_A * PANEL
    row_place = lax.axis_index("row")
    col_place = lax.axis_index("col")
    panel = spread(matrix[:, :order], "col", 0)
    joined = spread(jnp.concatenate([matrix[:order], other[:order], panel[:order]], 1), "row", 0)
    rows = joined[:, : local_cols + other_cols]
    block = joined[:, local_cols + other_cols :].T
    places = row_place * local_rows + jnp.arange(local_rows, dtype=jnp.int32)
    swept, eye = sweep_panel(block, panel.T, places)
    solved = eye - swept
    new_matrix = matrix - mul(solved, rows[:, :local_cols], ((0,), (0,)), CLOSE)
    new_other = other - mul(solved, rows[:, local_cols:], ((0,), (0,)), CLOSE)
    front = jnp.where(col_place == 0, swept.T, new_matrix[:, :order])
    return (new_matrix.at[:, :order].set(front), new_other)


def b_sweep(matrix, row_count, col_count):
    local_rows, local_cols = matrix.shape
    order = min(local_rows, local_cols)
    steps = STEPS_B * PANEL // order
    row_part = order // row_count
    col_part = order // col_count
    row_place = lax.axis_index("row")
    col_place = lax.axis_index("col")
    dealt = matrix.T.reshape(local_cols // order, col_count, col_part, local_rows)
    dealt = lax.all_to_all(dealt, "col", 1, 0, tiled=True).reshape(local_cols, local_rows)
    dealt = dealt.T.reshape(local_rows // order, row_count, row_part, local_cols)
    dealt = lax.all_to_all(dealt, "row", 1, 0, tiled=True).reshape(local_rows, local_cols)
    index = jnp.arange(local_rows, dtype=jnp.int32)
    for step in range(steps):
        top = step * row_part
        left = step * col_part
        panel = lax.all_gather(dealt[:, left : left + col_part].T, "col", axis=0, tiled=True)
        joined = jnp.concatenate([dealt[top : top + row_part], panel[:, top : top + row_part].T], 1)
        joined = lax.all_gather(joined, "row", axis=0, tiled=True)
        rows = joined[:, :local_cols]
        block = joined[:, local_cols:].T
        inside = (index >= top) & (index < top + row_part)
        places = jnp.where(inside, index - top + row_place * row_part, -1)
        swept, eye = sweep_panel(block, panel, places)
        updated = dealt + mul(swept - eye, rows, ((0,), (0,)), CLOSE)
        own = lax.dynamic_slice_in_dim(swept, col_place * col_part, col_part, 0).T
        dealt = updated.at[:, left : left + col_part].set(own)
    back = dealt.reshape(steps, 1, row_part, local_cols)
    back = lax.all_to_all(back, "row", 0, 1, tiled=True).reshape(local_rows, local_cols)
    back = back.T.reshape(steps, 1, col_part, local_rows)
    back = lax.all_to_all(back, "col", 0, 1, tiled=True).reshape(local_cols, local_rows)
    return back.T


def solution(mesh):
    row_count = mesh.shape["row"]
    col_count = mesh.shape["col"]

    def body(a_matrix, b_matrix, c_matrix):
        b_local = jnp.sum(b_matrix * b_matrix)
        a_swept, c_swept = a_sweep(a_matrix, c_matrix)
        b_inverse = b_sweep(b_matrix, row_count, col_count)
        inv_local = jnp.sum(b_inverse * b_inverse)
        sums = lax.psum(jnp.stack([b_local, inv_local]), ("row", "col"))
        scale = jnp.sqrt(jnp.sqrt(sums[1] / sums[0]))
        b_next = 0.5 * (scale * b_matrix + b_inverse / scale)
        return (a_swept, c_swept, b_next)

    return jax.shard_map(
        body,
        mesh=mesh,
        in_specs=(P("row", "col"), P("row", "col"), P("row", "col")),
        out_specs=(P("row", "col"), P("row", "col"), P("row", "col")),
        check_vma=False,
    )
```

profile of v0, /device:TPU:10, one launch (start us, length us, event | category | flops | bytes accessed | tf_op | source)
XLA Modules:
  0.0 1504.4 jit_solution(638320156755108339)
XLA Ops:
  9.2 29.3 %all_to_all.48 = f32[1,8,64,1024]{3,2,0,1:T(8,128)} all-to-all(f32[1,8,64,1024]{3,2,0,1:T(8,128)S(1)} %bitcast.702), channel_id=1, replica_groups=mesh['row'=4,'col'=8] {'col'}, dimensions={1} | all-to-all | bytes 4194304 | tf_op jit(solution)/shard_map/all_to_all | solution.py:82
  40.6 51.6 %all_to_all.49 = f32[2,4,128,512]{3,2,0,1:T(8,128)S(1)} all-to-all(f32[2,4,128,512]{3,2,0,1:T(8,128)S(1)} %copy.155), channel_id=1, replica_groups=mesh['row'=4,'col'=8] {'row'}, dimensions={1} | all-to-all | bytes 4194304 | tf_op jit(solution)/shard_map/all_to_all | solution.py:84
  93.5 27.3 %all-gather.17.cloned.1.call-done = f32[512,1024]{1,0:T(8,128)} async-done(((f32[64,1024]{1,0:T(8,128)}), f32[512,1024]{1,0:T(8,128)}) %all-gather.17.cloned.1.call-update) | async-done | bytes 2097168 | tf_op jit(solution)/shard_map/all_gather | solution.py:89
  125.3 42.9 %all-gather.19.cloned.1.call-done = f32[512,1024]{1,0:T(8,128)} async-done(((f32[128,1024]{1,0:T(8,128)}), f32[512,1024]{1,0:T(8,128)}) %all-gather.19.cloned.1.call-update) | async-done | bytes 2097168 | tf_op jit(solution)/shard_map/all_gather | solution.py:91
  182.8 3.3 convolution_subtract_fusion.8
  203.7 3.9 fusion.123
  221.2 3.5 scatter.31
  227.9 27.0 %all-gather.21.cloned.1.call-done = f32[512,1024]{1,0:T(8,128)} async-done(((f32[64,1024]{1,0:T(8,128)}), f32[512,1024]{1,0:T(8,128)}) %all-gather.21.cloned.1.call-update) | async-done | bytes 2097168 | tf_op jit(solution)/shard_map/all_gather | solution.py:89
  258.9 43.4 %all-gather.23.cloned.1.call-done = f32[512,1024]{1,0:T(8,128)} async-done(((f32[128,1024]{1,0:T(8,128)}), f32[512,1024]{1,0:T(8,128)}) %all-gather.23.cloned.1.call-update) | async-done | bytes 2097168 | tf_op jit(solution)/shard_map/all_gather | solution.py:91
  316.9 3.3 convolution_subtract_fusion.7
  337.5 3.9 fusion.121
  355.2 3.9 scatter.34
  362.1 27.0 %all-gather.25.cloned.1.call-done = f32[512,1024]{1,0:T(8,128)} async-done(((f32[64,1024]{1,0:T(8,128)}), f32[512,1024]{1,0:T(8,128)}) %all-gather.25.cloned.1.call-update) | async-done | bytes 2097168 | tf_op jit(solution)/shard_map/all_gather | solution.py:89
  393.4 43.2 %all-gather.27.cloned.1.call-done = f32[512,1024]{1,0:T(8,128)} async-done(((f32[128,1024]{1,0:T(8,128)}), f32[512,1024]{1,0:T(8,128)}) %all-gather.27.cloned.1.call-update) | async-done | bytes 2097168 | tf_op jit(solution)/shard_map/all_gather | solution.py:91
  451.1 3.3 convolution_subtract_fusion.6
  471.7 3.9 fusion.119
  489.3 3.5 scatter.35
  495.9 27.0 %all-gather.29.cloned.1.call-done = f32[512,1024]{1,0:T(8,128)} async-done(((f32[64,1024]{1,0:T(8,128)}), f32[512,1024]{1,0:T(8,128)}) %all-gather.29.cloned.1.call-update) | async-done | bytes 2097168 | tf_op jit(solution)/shard_map/all_gather | solution.py:89
  527.0 43.3 %all-gather.31.cloned.1.call-done = f32[512,1024]{1,0:T(8,128)} async-done(((f32[128,1024]{1,0:T(8,128)}), f32[512,1024]{1,0:T(8,128)}) %all-gather.31.cloned.1.call-update) | async-done | bytes 2097168 | tf_op jit(solution)/shard_map/all_gather | solution.py:91
  584.9 3.3 convolution_subtract_fusion.5
  605.7 3.9 fusion.117
  623.4 3.9 scatter.36
  630.3 27.0 %all-gather.33.cloned.1.call-done = f32[512,1024]{1,0:T(8,128)} async-done(((f32[64,1024]{1,0:T(8,128)}), f32[512,1024]{1,0:T(8,128)}) %all-gather.33.cloned.1.call-update) | async-done | bytes 2097168 | tf_op jit(solution)/shard_map/all_gather | solution.py:89
  661.3 43.4 %all-gather.35.cloned.1.call-done = f32[512,1024]{1,0:T(8,128)} async-done(((f32[128,1024]{1,0:T(8,128)}), f32[512,1024]{1,0:T(8,128)}) %all-gather.35.cloned.1.call-update) | async-done | bytes 2097168 | tf_op jit(solution)/shard_map/all_gather | solution.py:91
  719.3 3.3 convolution_subtract_fusion.4
  739.9 3.9 fusion.115
  757.4 3.5 scatter.39
  764.1 27.0 %all-gather.37.cloned.1.call-done = f32[512,1024]{1,0:T(8,128)} async-done(((f32[64,1024]{1,0:T(8,128)}), f32[512,1024]{1,0:T(8,128)}) %all-gather.37.cloned.1.call-update) | async-done | bytes 2097168 | tf_op jit(solution)/shard_map/all_gather | solution.py:89
  795.3 43.2 %all-gather.39.cloned.1.call-done = f32[512,1024]{1,0:T(8,128)} async-done(((f32[128,1024]{1,0:T(8,128)}), f32[512,1024]{1,0:T(8,128)}) %all-gather.39.cloned.1.call-update) | async-done | bytes 2097168 | tf_op jit(solution)/shard_map/all_gather | solution.py:91
  853.1 3.3 convolution_subtract_fusion.3
  873.7 3.9 fusion.113
  891.3 3.9 scatter.40
  897.3 4.7 slice_select_fusion
  903.0 22.2 %all-gather.41.cloned.1.call-done = f32[512,1024]{1,0:T(8,128)} async-done(((f32[64,1024]{1,0:T(8,128)}), f32[512,1024]{1,0:T(8,128)}) %all-gather.41.cloned.1.call-update) | async-done | bytes 2097168 | tf_op jit(solution)/shard_map/all_gather | solution.py:89
  936.7 73.2 %all-reduce.3.cloned.1.call-done = f32[2048,512]{1,0:T(8,128)} async-done(((f32[2048,512]{1,0:T(8,128)}), f32[2048,512]{1,0:T(8,128)}) %all-reduce.3.cloned.1.call-update) | async-done | bytes 4194320 | tf_op jit(solution)/shard_map/psum | solution.py:16
  1011.7 3.6 maximum_select_fusion
  1015.8 39.9 %all-gather.43.cloned.1.call-done = f32[512,1024]{1,0:T(8,128)} async-done(((f32[128,1024]{1,0:T(8,128)}), f32[512,1024]{1,0:T(8,128)}) %all-gather.43.cloned.1.call-update) | async-done | bytes 2097168 | tf_op jit(solution)/shard_map/all_gather | solution.py:91
  1081.7 3.1 copy.207
  1090.9 3.9 fusion.111
  1097.8 3.5 slice_subtract_fusion.15
  1121.3 90.3 %all-reduce.5.cloned.1.call-done = f32[512,2048]{1,0:T(8,128)} async-done(((f32[512,2048]{1,0:T(8,128)}), f32[512,2048]{1,0:T(8,128)}) %all-reduce.5.cloned.1.call-update) | async-done | bytes 4194320 | tf_op jit(solution)/shard_map/psum | solution.py:16
  1223.5 18.7 %all-gather.45.cloned.1.call-done = f32[512,1024]{1,0:T(8,128)} async-done(((f32[64,1024]{1,0:T(8,128)}), f32[512,1024]{1,0:T(8,128)}) %all-gather.45.cloned.1.call-update) | async-done | bytes 2097168 | tf_op jit(solution)/shard_map/all_gather | solution.py:89
  1242.1 3.3 copy.213
  1251.4 7.1 fusion.13
  1270.0 22.7 %all-gather.47.cloned.1.call-done = f32[512,1024]{1,0:T(8,128)} async-done(((f32[128,1024]{1,0:T(8,128)}), f32[512,1024]{1,0:T(8,128)}) %all-gather.47.cloned.1.call-update) | async-done | bytes 2097168 | tf_op jit(solution)/shard_map/all_gather | solution.py:91
  1307.5 3.3 convolution_subtract_fusion.1
  1310.8 3.1 copy.215
  1328.2 3.9 fusion.109
  1341.9 3.2 fusion.53
  1345.1 3.4 scatter.44
  1348.6 6.7 all-to-all-start.2
  1356.6 3.3 copy.148
  1359.9 3.5 slice.808
  1367.4 7.8 fusion.15
  1375.2 3.4 copy.151
  1378.5 5.6 slice_subtract_fusion.3
  1385.7 4.6 fusion.234
  1390.3 9.9 all-to-all-done.2
  1403.9 5.1 all-to-all-start.3
  1409.1 3.0 slice_subtract_fusion.1
  1414.6 11.6 convolution_subtract_fusion
  1426.3 5.8 fusion.2
  1438.4 9.8 convolution_subtract_fusion.9
  1448.2 42.8 %psum.23 = f32[2]{0:T(128)S(1)} all-reduce(f32[2]{0:T(128)S(1)} %pad_maximum_fusion.35), channel_id=1, replica_groups=mesh['row'=4,'col'=8] {'row','col'}, use_global_device_ids=true, to_apply=%region_66.67 | all-reduce | flops 2 | bytes 16 | tf_op jit(solution)/shard_map/psum | solution.py:116
  (720 shorter events, 469.2 us)
Async XLA Ops:
  7.2 113.7 %all-gather.17.cloned.1.call-start = ((), (), s32[]{:S(2)}) async-start(), calls=%async_computation.6 | async-start | bytes 2359296 | tf_op jit(solution)/shard_map/all_gather | solution.py:89
  9.1 29.3 %copy-start.55 = (f32[1024,512]{0,1:T(8,128)}, f32[1024,512]{0,1:T(8,128)S(1)}, u32[]{:S(2)}) copy-start(f32[1024,512]{0,1:T(8,128)S(1)} %copy.152) | copy-start | bytes 6291460
  93.3 74.9 %all-gather.19.cloned.1.call-start = ((), (), s32[]{:S(2)}) async-start(), calls=%async_computation.7 | async-start | bytes 2621440 | tf_op jit(solution)/shard_map/all_gather | solution.py:91
  123.7 131.2 %all-gather.21.cloned.1.call-start = ((), (), s32[]{:S(2)}) async-start(), calls=%async_computation.8 | async-start | bytes 2359296 | tf_op jit(solution)/shard_map/all_gather | solution.py:89
  171.9 3.6 copy-start.21
  195.3 5.5 copy-start.12
  210.6 2.8 copy-start.88
  226.9 75.4 %all-gather.23.cloned.1.call-start = ((), (), s32[]{:S(2)}) async-start(), calls=%async_computation.9 | async-start | bytes 2621440 | tf_op jit(solution)/shard_map/all_gather | solution.py:91
  257.8 131.3 %all-gather.25.cloned.1.call-start = ((), (), s32[]{:S(2)}) async-start(), calls=%async_computation.10 | async-start | bytes 2359296 | tf_op jit(solution)/shard_map/all_gather | solution.py:89
  306.0 3.6 copy-start.23
  329.4 5.5 copy-start.13
  344.5 2.8 copy-start.89
  361.1 75.4 %all-gather.27.cloned.1.call-start = ((), (), s32[]{:S(2)}) async-start(), calls=%async_computation.11 | async-start | bytes 2621440 | tf_op jit(solution)/shard_map/all_gather | solution.py:91
  392.0 130.9 %all-gather.29.cloned.1.call-start = ((), (), s32[]{:S(2)}) async-start(), calls=%async_computation.12 | async-start | bytes 2359296 | tf_op jit(solution)/shard_map/all_gather | solution.py:89
  440.3 3.6 copy-start.25
  463.6 5.5 copy-start.14
  478.7 2.8 copy-start.90
  494.9 75.4 %all-gather.31.cloned.1.call-start = ((), (), s32[]{:S(2)}) async-start(), calls=%async_computation.13 | async-start | bytes 2621440 | tf_op jit(solution)/shard_map/all_gather | solution.py:91
  525.8 131.5 %all-gather.33.cloned.1.call-start = ((), (), s32[]{:S(2)}) async-start(), calls=%async_computation.14 | async-start | bytes 2359296 | tf_op jit(solution)/shard_map/all_gather | solution.py:89
  574.0 3.6 copy-start.27
  597.4 5.5 copy-start.15
  612.7 2.8 copy-start.91
  629.2 75.4 %all-gather.35.cloned.1.call-start = ((), (), s32[]{:S(2)}) async-start(), calls=%async_computation.15 | async-start | bytes 2621440 | tf_op jit(solution)/shard_map/all_gather | solution.py:91
  660.2 130.9 %all-gather.37.cloned.1.call-start = ((), (), s32[]{:S(2)}) async-start(), calls=%async_computation.16 | async-start | bytes 2359296 | tf_op jit(solution)/shard_map/all_gather | solution.py:89
  708.4 3.6 copy-start.29
  731.8 5.5 copy-start.16
  746.8 2.8 copy-start.92
  763.1 75.4 %all-gather.39.cloned.1.call-start = ((), (), s32[]{:S(2)}) async-start(), calls=%async_computation.17 | async-start | bytes 2621440 | tf_op jit(solution)/shard_map/all_gather | solution.py:91
  794.0 131.3 %all-gather.41.cloned.1.call-start = ((), (), s32[]{:S(2)}) async-start(), calls=%async_computation.18 | async-start | bytes 2359296 | tf_op jit(solution)/shard_map/all_gather | solution.py:89
  842.2 3.6 copy-start.31
  865.6 5.5 copy-start.17
  880.6 2.8 copy-start.93
  897.2 112.6 %all-reduce.3.cloned.1.call-start = ((), (), s32[]{:S(2)}) async-start(), calls=%async_computation.4 | async-start | bytes 8388608 | tf_op jit(solution)/shard_map/psum | solution.py:16
  902.0 153.7 %all-gather.43.cloned.1.call-start = ((), (), s32[]{:S(2)}) async-start(), calls=%async_computation.19 | async-start | bytes 2621440 | tf_op jit(solution)/shard_map/all_gather | solution.py:91
  928.1 283.5 %all-reduce.5.cloned.1.call-start = ((), (), s32[]{:S(2)}) async-start(), calls=%async_computation.5 | async-start | bytes 8388608 | tf_op jit(solution)/shard_map/psum | solution.py:16
  928.7 5.8 copy-start.107
  1015.3 226.8 %all-gather.45.cloned.1.call-start = ((), (), s32[]{:S(2)}) async-start(), calls=%async_computation.20 | async-start | bytes 2359296 | tf_op jit(solution)/shard_map/all_gather | solution.py:89
  1059.5 3.6 copy-start.33
  1063.5 2.9 copy-start.43
  1064.4 2.5 copy-start
  1084.8 4.5 copy-start.19
  1087.6 3.3 copy-start.1
  1097.8 3.5 copy-start.85
  1097.8 3.8 copy-start.94
  1103.1 2.6 copy-start.66
  1117.7 174.9 %all-gather.47.cloned.1.call-start = ((), (), s32[]{:S(2)}) async-start(), calls=%async_computation.21 | async-start | bytes 2621440 | tf_op jit(solution)/shard_map/all_gather | solution.py:91
  1215.4 3.6 copy-start.38
  1248.2 3.2 copy-start.39
  1251.4 7.1 copy-start.36
  1296.4 3.8 copy-start.35
  1320.1 5.5 copy-start.11
  1335.1 2.8 copy-start.87
  1348.6 51.7 %all-to-all-start.2 = ((f32[8,1,128,512]{3,2,1,0:T(8,128)}), f32[8,1,128,512]{3,2,1,0:T(8,128)}, u32[]{:S(2)}, u32[]{:S(2)}) async-start(f32[8,1,128,512]{3,2,1,0:T(8,128)} %bitcast.706), calls=%async_computation.2 | async-start | bytes 4194304 | tf_op jit(solution)/shard_map/all_to_all | solution.py:101
  1356.6 10.8 slice-start
  1359.9 7.5 slice-start.1
  1375.2 3.4 copy-start.97
  1378.5 7.2 copy-start.7
  1378.5 7.2 copy-start.8
  1403.9 8.2 slice-start.2
  1403.9 30.3 %all-to-all-start.3 = ((f32[8,1,64,1024]{3,2,1,0:T(8,128)}), f32[8,1,64,1024]{3,2,1,0:T(8,128)}, u32[]{:S(2)}, u32[]{:S(2)}) async-start(f32[8,1,64,1024]{3,2,1,0:T(8,128)} %bitcast.72), calls=%async_computation.3 | async-start | bytes 4194304 | tf_op jit(solution)/shard_map/all_to_all | solution.py:103
  1409.1 3.8 slice-start.3
  1409.1 5.5 copy-start.4
  1412.2 14.1 copy-start.3
  1426.3 12.1 copy-start.5
  (69 other events, 118.0 us)
Sparse Core Ops, SparseCore 0:
  93.5 27.2 all-gather.16
  123.8 44.3 all-gather.18
  227.0 27.8 all-gather.20
  257.9 44.3 all-gather.22
  361.2 27.8 all-gather.24
  392.2 44.3 all-gather.26
  495.0 27.8 all-gather.28
  525.9 44.3 all-gather.30
  629.4 27.8 all-gather.32
  660.3 44.3 all-gather.34
  763.2 27.8 all-gather.36
  794.1 44.3 all-gather.38
  897.3 27.8 all-gather.40
  928.9 80.8 all-reduce.2
  1011.2 44.4 all-gather.42
  1058.5 153.1 all-reduce.4
  1213.4 28.6 all-gather.44
  1248.3 44.3 all-gather.46
where the time goes:
time: 1520 us; the launch traced here: 1500 us
  waiting for transfers between devices  701 us (46%)
  matrix products  290 us (19%)
  local copies, waits for them, and re-layouts  229 us (15%)
  blocking collectives  124 us (8%)
  other arithmetic  115 us (8%)
  between operations  31.5 us (2%)
    all_gather x8, waiting for transfers between devices, b_sweep(): joined = lax.all_gather(joined, 'row', axis=0, tiled=True)  322 us
    all_gather x8, waiting for transfers between devices, b_sweep(): lax.all_gather(dealt[:, left:left + col_part].T, 'col', axis=0, tiled=True)  203 us
    psum x2, waiting for transfers between devices, spread(): return lax.psum(kept, axis)  163 us
    dot_general x46, matrix products, mul(): lax.dot_general(left, right, (dims, ((), ())), precision=precision, prefe...  149 us
    dot_general x108, matrix products, pivot_inverse(): jnp.dot(unit, approx, precision=EXACT, preferred_element_type=jnp.float32)  97.6 us
    unnamed x226, local copies, waits for them, and re-layouts  55.5 us
    dot_general x18, local copies, waits for them, and re-layouts, mul(): lax.dot_general(left, right, (dims, ((), ())), precision=precision, prefe...  55.2 us
    all_to_all x1, blocking collectives, b_sweep(): lax.all_to_all(dealt, 'row', 1, 0, tiled=True)  51.6 us
  transfers between devices with their start and end apart: 20, of which 20 were waited for; matrix products, arithmetic and copies ran while one was open for 12% of the time, Pallas kernels for 0%

commit v1 on v0

--- a/solution.py
+++ b/solution.py
@@ -88,7 +88,14 @@
         left = step * col_part
         panel = lax.all_gather(dealt[:, left : left + col_part].T, "col", axis=0, tiled=True)
         joined = jnp.concatenate([dealt[top : top + row_part], panel[:, top : top + row_part].T], 1)
-        joined = lax.all_gather(joined, "row", axis=0, tiled=True)
+        ring = [joined]
+        for hop in range(3):
+            ring.append(lax.ppermute(ring[-1], "row", [(dev, (dev + 1) % 4) for dev in range(4)]))
+        joined = jnp.roll(
+            jnp.concatenate(ring[::-1], axis=0),
+            (lax.axis_index("row") + 1) * ring[0].shape[0],
+            axis=0,
+        )
         rows = joined[:, :local_cols]
         block = joined[:, local_cols:].T
         inside = (index >= top) & (index < top + row_part)

time: 1520 us -> 1470 us (0.967)
  waiting for transfers between devices: 701 us -> 609 us
  starting transfers between devices: 13 us -> 44.4 us
  other arithmetic: 115 us -> 136 us
    all_gather x8 -> x0, waiting for transfers between devices: 322 us -> none  [b_sweep(): joined = lax.all_gather(joined, 'row', axis=0, tiled=True)]
    ppermute x0 -> x24, waiting for transfers between devices: none -> 266 us  [b_sweep(): lax.ppermute(ring[-1], 'row', [(dev, (dev + 1) % 4) for dev in range(4)])]
    ppermute x0 -> x24, starting transfers between devices: none -> 31.5 us  [b_sweep(): lax.ppermute(ring[-1], 'row', [(dev, (dev + 1) % 4) for dev in range(4)])]
    concatenate x0 -> x8, other arithmetic: none -> 28.6 us  [b_sweep(): jnp.roll(jnp.concatenate(ring[::-1], axis=0), (lax.axis_index('row') + 1)...]
    psum x2, waiting for transfers between devices: 163 us -> 136 us  [spread(): return lax.psum(kept, axis)]
    unnamed x226 -> x260, local copies, waits for them, and re-layouts: 55.5 us -> 65.1 us
  transfers between devices with their start and end apart: 20 -> 36, of which waited for: 20 -> 35; matrix products, arithmetic and copies ran while one was open for 12% -> 12% of each run, Pallas kernels for 0% -> 0%
where the time goes in v1:
time: 1470 us
  waiting for transfers between devices  609 us (41%)
  matrix products  294 us (20%)
  local copies, waits for them, and re-layouts  228 us (16%)
  other arithmetic  136 us (9%)
  blocking collectives  124 us (8%)
  starting transfers between devices  44.4 us (3%)
  between operations  31 us (2%)
    ppermute x24, waiting for transfers between devices, b_sweep(): lax.ppermute(ring[-1], 'row', [(dev, (dev + 1) % 4) for dev in range(4)])  266 us
    all_gather x8, waiting for transfers between devices, b_sweep(): lax.all_gather(dealt[:, left:left + col_part].T, 'col', axis=0, tiled=True)  196 us
    dot_general x46, matrix products, mul(): lax.dot_general(left, right, (dims, ((), ())), precision=precision, prefe...  157 us
    psum x2, waiting for transfers between devices, spread(): return lax.psum(kept, axis)  136 us
    dot_general x108, matrix products, pivot_inverse(): jnp.dot(unit, approx, precision=EXACT, preferred_element_type=jnp.float32)  94.2 us
    unnamed x260, local copies, waits for them, and re-layouts  65.1 us
    dot_general x18, local copies, waits for them, and re-layouts, mul(): lax.dot_general(left, right, (dims, ((), ())), precision=precision, prefe...  55.2 us
    all_to_all x1, blocking collectives, b_sweep(): lax.all_to_all(dealt, 'row', 1, 0, tiled=True)  51.6 us
  transfers between devices with their start and end apart: 36, of which 35 were waited for; matrix products, arithmetic and copies ran while one was open for 12% of the time, Pallas kernels for 0%

profile of v1, /device:TPU:10, one launch (start us, length us, event | category | flops | bytes accessed | tf_op | source)
XLA Modules:
  0.0 1465.5 jit_solution(18119118820186917541)
XLA Ops:
  9.2 29.3 %all_to_all.48 = f32[1,8,64,1024]{3,2,0,1:T(8,128)} all-to-all(f32[1,8,64,1024]{3,2,0,1:T(8,128)S(1)} %bitcast.702), channel_id=1, replica_groups=mesh['row'=4,'col'=8] {'col'}, dimensions={1} | all-to-all | bytes 4194304 | tf_op jit(solution)/shard_map/all_to_all | solution.py:82
  40.6 51.6 %all_to_all.49 = f32[2,4,128,512]{3,2,0,1:T(8,128)S(1)} all-to-all(f32[2,4,128,512]{3,2,0,1:T(8,128)S(1)} %copy.155), channel_id=1, replica_groups=mesh['row'=4,'col'=8] {'row'}, dimensions={1} | all-to-all | bytes 4194304 | tf_op jit(solution)/shard_map/all_to_all | solution.py:84
  93.5 27.3 %all-gather.9.cloned.1.call-done = f32[512,1024]{1,0:T(8,128)} async-done(((f32[64,1024]{1,0:T(8,128)}), f32[512,1024]{1,0:T(8,128)}) %all-gather.9.cloned.1.call-update) | async-done | bytes 2097168 | tf_op jit(solution)/shard_map/all_gather | solution.py:89
  124.4 12.6 collective-permute-done
  139.8 11.1 collective-permute-done.1
  152.2 13.2 collective-permute-done.2
  165.4 4.0 fusion.109
  184.1 3.7 convolution_subtract_fusion.8
  204.8 3.9 fusion.195
  229.3 27.1 %all-gather.11.cloned.1.call-done = f32[512,1024]{1,0:T(8,128)} async-done(((f32[64,1024]{1,0:T(8,128)}), f32[512,1024]{1,0:T(8,128)}) %all-gather.11.cloned.1.call-update) | async-done | bytes 2097168 | tf_op jit(solution)/shard_map/all_gather | solution.py:89
  260.0 12.6 collective-permute-done.3
  275.4 11.0 collective-permute-done.4
  287.6 13.0 collective-permute-done.5
  318.4 3.7 convolution_subtract_fusion.7
  339.1 3.9 fusion.193
  357.2 3.9 scatter.34
  364.1 27.1 %all-gather.13.cloned.1.call-done = f32[512,1024]{1,0:T(8,128)} async-done(((f32[64,1024]{1,0:T(8,128)}), f32[512,1024]{1,0:T(8,128)}) %all-gather.13.cloned.1.call-update) | async-done | bytes 2097168 | tf_op jit(solution)/shard_map/all_gather | solution.py:89
  394.8 12.6 collective-permute-done.6
  409.5 11.6 collective-permute-done.7
  422.3 13.0 collective-permute-done.8
  453.1 3.7 convolution_subtract_fusion.6
  473.9 3.9 fusion.191
  498.4 27.1 %all-gather.15.cloned.1.call-done = f32[512,1024]{1,0:T(8,128)} async-done(((f32[64,1024]{1,0:T(8,128)}), f32[512,1024]{1,0:T(8,128)}) %all-gather.15.cloned.1.call-update) | async-done | bytes 2097168 | tf_op jit(solution)/shard_map/all_gather | solution.py:89
  529.0 12.6 collective-permute-done.9
  543.8 11.6 collective-permute-done.10
  556.6 13.0 collective-permute-done.11
  608.1 3.9 fusion.189
  626.1 3.9 scatter.36
  633.0 27.1 %all-gather.17.cloned.1.call-done = f32[512,1024]{1,0:T(8,128)} async-done(((f32[64,1024]{1,0:T(8,128)}), f32[512,1024]{1,0:T(8,128)}) %all-gather.17.cloned.1.call-update) | async-done | bytes 2097168 | tf_op jit(solution)/shard_map/all_gather | solution.py:89
  663.7 12.6 collective-permute-done.12
  678.4 11.6 collective-permute-done.13
  691.2 13.0 collective-permute-done.14
  742.8 3.9 fusion.187
  767.3 27.1 %all-gather.19.cloned.1.call-done = f32[512,1024]{1,0:T(8,128)} async-done(((f32[64,1024]{1,0:T(8,128)}), f32[512,1024]{1,0:T(8,128)}) %all-gather.19.cloned.1.call-update) | async-done | bytes 2097168 | tf_op jit(solution)/shard_map/all_gather | solution.py:89
  798.0 12.6 collective-permute-done.15
  812.7 11.6 collective-permute-done.16
  825.5 13.0 collective-permute-done.17
  877.1 3.9 fusion.185
  895.0 3.9 scatter.40
  901.0 4.7 slice_select_fusion
  906.7 22.3 %all-gather.21.cloned.1.call-done = f32[512,1024]{1,0:T(8,128)} async-done(((f32[64,1024]{1,0:T(8,128)}), f32[512,1024]{1,0:T(8,128)}) %all-gather.21.cloned.1.call-update) | async-done | bytes 2097168 | tf_op jit(solution)/shard_map/all_gather | solution.py:89
  935.5 9.7 collective-permute-done.18
  948.6 10.5 collective-permute-done.19
  965.3 48.5 %all-reduce.3.cloned.1.call-done = f32[2048,512]{1,0:T(8,128)} async-done(((f32[2048,512]{1,0:T(8,128)}), f32[2048,512]{1,0:T(8,128)}) %all-reduce.3.cloned.1.call-update) | async-done | bytes 4194320 | tf_op jit(solution)/shard_map/psum | solution.py:16
  1019.4 3.9 fusion.55
  1058.0 3.9 fusion.183
  1085.1 87.5 %all-reduce.5.cloned.1.call-done = f32[512,2048]{1,0:T(8,128)} async-done(((f32[512,2048]{1,0:T(8,128)}), f32[512,2048]{1,0:T(8,128)}) %all-reduce.5.cloned.1.call-update) | async-done | bytes 4194320 | tf_op jit(solution)/shard_map/psum | solution.py:16
  1183.2 7.8 fusion.13
  1192.0 11.0 all-gather.23.cloned.1.call-done
  1209.3 5.7 fusion
  1226.8 9.4 collective-permute-done.22
  1239.2 11.1 collective-permute-done.23
  1250.3 4.8 fusion.46
  1290.6 3.9 fusion.181
  1311.0 7.2 all-to-all-start.2
  1330.4 7.7 fusion.15
  1341.5 5.6 slice_subtract_fusion.3
  1348.6 4.6 fusion.306
  1353.2 8.0 all-to-all-done.2
  1364.9 5.2 all-to-all-start.3
  1375.7 11.6 convolution_subtract_fusion
  1387.3 5.8 fusion.2
  1399.4 9.8 convolution_subtract_fusion.9
  1409.2 42.8 %psum.23 = f32[2]{0:T(128)S(1)} all-reduce(f32[2]{0:T(128)S(1)} %pad_maximum_fusion.35), channel_id=1, replica_groups=mesh['row'=4,'col'=8] {'row','col'}, use_global_device_ids=true, to_apply=%region_66.68 | all-reduce | flops 2 | bytes 16 | tf_op jit(solution)/shard_map/psum | solution.py:123
  (787 shorter events, 565.3 us)
Async XLA Ops:
  7.2 113.6 %all-gather.9.cloned.1.call-start = ((), (), s32[]{:S(2)}) async-start(), calls=%async_computation.6 | async-start | bytes 2359296 | tf_op jit(solution)/shard_map/all_gather | solution.py:89
  9.1 29.3 %copy-start.53 = (f32[1024,512]{0,1:T(8,128)}, f32[1024,512]{0,1:T(8,128)S(1)}, u32[]{:S(2)}) copy-start(f32[1024,512]{0,1:T(8,128)S(1)} %copy.152) | copy-start | bytes 6291460
  93.3 163.2 %all-gather.11.cloned.1.call-start = ((), (), s32[]{:S(2)}) async-start(), calls=%async_computation.7 | async-start | bytes 2359296 | tf_op jit(solution)/shard_map/all_gather | solution.py:89
  122.7 29.2 %copy-start.38 = (f32[512,1024]{0,1:T(8,128)}, f32[512,1024]{0,1:T(8,128)S(1)}, u32[]{:S(2)}) copy-start(f32[512,1024]{0,1:T(8,128)S(1)} %copy.157) | copy-start | bytes 6291460
  122.8 29.1 %copy-start.113 = (f32[128,512]{1,0:T(8,128)}, f32[128,512]{1,0:T(8,128)S(1)}, u32[]{:S(2)}) copy-start(f32[128,512]{1,0:T(8,128)S(1)} %slice_bitcast_fusion.40) | copy-start | bytes 786436
  122.8 14.1 collective-permute-start
  136.9 15.0 %copy-start.120 = (f32[128,1024]{1,0:T(8,128)}, f32[128,1024]{1,0:T(8,128)S(1)}, u32[]{:S(2)}) copy-start(f32[128,1024]{1,0:T(8,128)S(1)} %collective-permute-done) | copy-start | bytes 1572868
  136.9 13.9 collective-permute-start.1
  150.9 14.5 collective-permute-start.2
  151.9 13.5 copy-start.114
  151.9 13.5 copy-start.121
  228.3 162.9 %all-gather.13.cloned.1.call-start = ((), (), s32[]{:S(2)}) async-start(), calls=%async_computation.8 | async-start | bytes 2359296 | tf_op jit(solution)/shard_map/all_gather | solution.py:89
  258.4 28.9 %copy-start.42 = (f32[512,1024]{0,1:T(8,128)}, f32[512,1024]{0,1:T(8,128)S(1)}, u32[]{:S(2)}) copy-start(f32[512,1024]{0,1:T(8,128)S(1)} %copy.165) | copy-start | bytes 6291460
  258.5 14.1 collective-permute-start.3
  272.6 13.8 collective-permute-start.4
  286.4 14.1 collective-permute-start.5
  331.2 5.5 copy-start.12
  363.0 162.4 %all-gather.15.cloned.1.call-start = ((), (), s32[]{:S(2)}) async-start(), calls=%async_computation.9 | async-start | bytes 2359296 | tf_op jit(solution)/shard_map/all_gather | solution.py:89
  393.1 28.9 %copy-start.45 = (f32[512,1024]{0,1:T(8,128)}, f32[512,1024]{0,1:T(8,128)S(1)}, u32[]{:S(2)}) copy-start(f32[512,1024]{0,1:T(8,128)S(1)} %copy.173) | copy-start | bytes 6291460
  393.2 14.1 collective-permute-start.6
  407.3 13.8 collective-permute-start.7
  421.1 14.1 collective-permute-start.8
  465.9 5.5 copy-start.13
  497.3 162.8 %all-gather.17.cloned.1.call-start = ((), (), s32[]{:S(2)}) async-start(), calls=%async_computation.10 | async-start | bytes 2359296 | tf_op jit(solution)/shard_map/all_gather | solution.py:89
  527.4 28.9 %copy-start.47 = (f32[512,1024]{0,1:T(8,128)}, f32[512,1024]{0,1:T(8,128)S(1)}, u32[]{:S(2)}) copy-start(f32[512,1024]{0,1:T(8,128)S(1)} %copy.181) | copy-start | bytes 6291460
  527.5 14.1 collective-permute-start.9
  541.6 13.8 collective-permute-start.10
  555.4 14.1 collective-permute-start.11
  632.0 162.4 %all-gather.19.cloned.1.call-start = ((), (), s32[]{:S(2)}) async-start(), calls=%async_computation.11 | async-start | bytes 2359296 | tf_op jit(solution)/shard_map/all_gather | solution.py:89
  662.1 28.9 %copy-start.49 = (f32[512,1024]{0,1:T(8,128)}, f32[512,1024]{0,1:T(8,128)S(1)}, u32[]{:S(2)}) copy-start(f32[512,1024]{0,1:T(8,128)S(1)} %copy.189) | copy-start | bytes 6291460
  662.1 14.1 collective-permute-start.12
  676.3 13.8 collective-permute-start.13
  690.1 14.1 collective-permute-start.14
  734.9 5.5 copy-start.15
  766.2 162.8 %all-gather.21.cloned.1.call-start = ((), (), s32[]{:S(2)}) async-start(), calls=%async_computation.12 | async-start | bytes 2359296 | tf_op jit(solution)/shard_map/all_gather | solution.py:89
  796.3 28.9 %copy-start.51 = (f32[512,1024]{0,1:T(8,128)}, f32[512,1024]{0,1:T(8,128)S(1)}, u32[]{:S(2)}) copy-start(f32[512,1024]{0,1:T(8,128)S(1)} %copy.197) | copy-start | bytes 6291460
  796.4 14.1 collective-permute-start.15
  810.5 13.8 collective-permute-start.16
  824.3 14.1 collective-permute-start.17
  900.9 112.9 %all-reduce.3.cloned.1.call-start = ((), (), s32[]{:S(2)}) async-start(), calls=%async_computation.4 | async-start | bytes 8388608 | tf_op jit(solution)/shard_map/psum | solution.py:16
  905.7 266.9 %all-reduce.5.cloned.1.call-start = ((), (), s32[]{:S(2)}) async-start(), calls=%async_computation.5 | async-start | bytes 8388608 | tf_op jit(solution)/shard_map/psum | solution.py:16
  931.1 15.6 %copy-start.124 = (s32[1536]{0:T(1024)S(1)}, s32[1536]{0:T(1024)}, u32[]{:S(2)}) copy-start(s32[1536]{0:T(1024)} %get-tuple-element.145) | copy-start | bytes 18436
  931.1 14.1 collective-permute-start.18
  935.5 24.6 %copy-start.123 = (s32[1536]{0:T(1024)S(1)}, s32[1536]{0:T(1024)}, u32[]{:S(2)}) copy-start(s32[1536]{0:T(1024)} %get-tuple-element.139) | copy-start | bytes 18436
  945.2 14.9 %copy-start.122 = (f32[128,1024]{1,0:T(8,128)}, f32[128,1024]{1,0:T(8,128)S(1)}, u32[]{:S(2)}) copy-start(f32[128,1024]{1,0:T(8,128)S(1)} %collective-permute-done.18) | copy-start | bytes 1572868
  945.2 13.9 collective-permute-start.19
  959.1 60.2 %collective-permute-start.20 = (f32[128,1024]{1,0:T(8,128)}, f32[128,1024]{1,0:T(8,128)}, u32[]{:S(2)}, u32[]{:S(2)}) collective-permute-start(f32[128,1024]{1,0:T(8,128)} %collective-permute-done.19), channel_id=1, source_target_pairs={{0,8},{8,16},{16,24},{24,0},{1,9},{9,17},{17,25},{25,1},{2,10},{10... | collective-permute-start | bytes 1572872 | tf_op jit(solution)/shard_map/ppermute | solution.py:93
  1019.3 183.7 %all-gather.23.cloned.1.call-start = ((), (), s32[]{:S(2)}) async-start(), calls=%async_computation.13 | async-start | bytes 2359296 | tf_op jit(solution)/shard_map/all_gather | solution.py:89
  1192.0 14.8 %copy-start.116 = (f32[128,512]{1,0:T(8,128)}, f32[128,512]{1,0:T(8,128)S(1)}, u32[]{:S(2)}) copy-start(f32[128,512]{1,0:T(8,128)S(1)} %slice.944) | copy-start | bytes 786436
  1207.8 14.4 collective-permute-start.21
  1218.9 31.4 %copy-start.117 = (f32[128,512]{1,0:T(8,128)S(1)}, f32[128,512]{1,0:T(8,128)}, u32[]{:S(2)}) copy-start(f32[128,512]{1,0:T(8,128)} %copy-done.116) | copy-start | bytes 786436
  1218.9 31.4 %copy-start.119 = (f32[128,512]{1,0:T(8,128)S(1)}, f32[128,512]{1,0:T(8,128)}, u32[]{:S(2)}) copy-start(f32[128,512]{1,0:T(8,128)} %copy-done.118) | copy-start | bytes 786436
  1222.2 14.0 collective-permute-start.22
  1236.2 14.1 collective-permute-start.23
  1311.0 50.2 %all-to-all-start.2 = ((f32[8,1,128,512]{3,2,1,0:T(8,128)}), f32[8,1,128,512]{3,2,1,0:T(8,128)}, u32[]{:S(2)}, u32[]{:S(2)}) async-start(f32[8,1,128,512]{3,2,1,0:T(8,128)} %bitcast.706), calls=%async_computation.2 | async-start | bytes 4194304 | tf_op jit(solution)/shard_map/all_to_all | solution.py:108
  1319.6 10.8 slice-start
  1322.9 7.5 slice-start.1
  1341.5 7.1 copy-start.7
  1341.5 7.1 copy-start.8
  1364.9 8.3 slice-start.2
  1364.9 30.4 %all-to-all-start.3 = ((f32[8,1,64,1024]{3,2,1,0:T(8,128)}), f32[8,1,64,1024]{3,2,1,0:T(8,128)}, u32[]{:S(2)}, u32[]{:S(2)}) async-start(f32[8,1,64,1024]{3,2,1,0:T(8,128)} %bitcast.72), calls=%async_computation.3 | async-start | bytes 4194304 | tf_op jit(solution)/shard_map/all_to_all | solution.py:110
  1370.2 5.5 copy-start.4
  1373.2 14.1 copy-start.3
  1387.3 12.1 copy-start.5
  (102 other events, 230.7 us)
Sparse Core Ops, SparseCore 0:
  93.5 27.2 all-gather.8
  228.4 28.0 all-gather.10
  363.2 27.9 all-gather.12
  497.5 27.9 all-gather.14
  632.1 27.9 all-gather.16
  766.4 27.9 all-gather.18
  901.0 27.9 all-gather.20
  932.9 80.8 all-reduce.2
  1019.4 153.0 all-reduce.4
  1174.3 28.6 all-gather.22
